TPU v7x, 32 devices: a whole 2x2x4 slice. The times are simulated.
32 devices in a mesh: chain: 8 (over y, x, core), par: 4 (over z).
Axes of the slice: x: 2, y: 2, z: 4, core: 2. Of those that a mesh axis runs over, the one named last changes fastest.
Arguments:
- propagation_gains: bfloat16 [4, 16, 64, 8192], P('par', None, None, 'chain'), may hold values from -0.13258252 to 0.13258252, as said below
- observed_samples: bfloat16 [4, 16, 32, 8192], P('par', None, None, 'chain'), may hold values from -6 to 6
- disturbance_variance: float32 [4, 16], P(None, 'chain'), may hold values from 0.05 to 0.5
- retained_branches: int32 [4, 16, 16, 1024], P(None, 'chain', 'par'), may hold values from 0 to 63
Outputs:
- distances: float32 [4, 16, 16, 1024], P(None, 'chain', 'par')
Inputs may be any that keep to these rules, and one draw needn't show every extreme that they name: `propagation_gains`: row 2u holds the real and row 2u+1 the imaginary part of the channel to user u.
All inputs are finite; a program needn't handle non-finite values.
Results may differ from a plain program's by a relative error of at most 0.0003.
Values sent between devices are 32-bit elements; how exact they have to be, the bound alone decides.
A program may use at most 64 MiB of HBM per device.

v0:
```python
import jax
import jax.numpy as jnp
from jax import lax
from jax.sharding import PartitionSpec as P

constellation_norm = 1.0 / 42.0**0.5


def prefix(x, axis, combine, identity):
    length, here = (lax.axis_size(axis), lax.axis_index(axis))
    everything = jax.tree.map(lambda part: lax.all_gather(part, axis), x)
    start = jax.tree.map(
        lambda part, zero: jnp.broadcast_to(jnp.asarray(zero, part.dtype), part.shape), x, identity
    )

    def turn(k, before):
        reached = k < here
        new = combine(before, jax.tree.map(lambda part: part[k], everything))
        return jax.tree.map(lambda a, b: jnp.where(reached, a, b), new, before)

    return lax.fori_loop(0, length, turn, start)


def from_root(block, axis, owner):
    block = jnp.where(lax.axis_index(axis) == owner, block, jnp.zeros_like(block))
    return lax.psum(block, axis)


def fold_stats(raw_gram, raw_cross):
    outer_dimensions = raw_gram.shape[:-2]
    terminal_number = raw_gram.shape[-1] // 2
    pieces = raw_gram.reshape(outer_dimensions + (terminal_number, 2, terminal_number, 2))
    same_part = pieces[..., :, 0, :, 0] + pieces[..., :, 1, :, 1]
    cross_part = pieces[..., :, 1, :, 0] - pieces[..., :, 0, :, 1]
    crossed = raw_cross.reshape(outer_dimensions + (terminal_number, 2, -1, 2))
    rhs_real = crossed[..., :, 0, :, 0] + crossed[..., :, 1, :, 1]
    rhs_imag = crossed[..., :, 0, :, 1] - crossed[..., :, 1, :, 0]
    rhs = jnp.stack([rhs_real, rhs_imag], axis=-2).reshape(
        outer_dimensions + (2 * terminal_number, -1)
    )
    return (same_part, cross_part, rhs)


def assemble(same_part, cross_part, noise):
    row_even = jnp.stack([same_part, cross_part], axis=-1)
    row_odd = jnp.stack([-cross_part, same_part], axis=-1)
    whole = jnp.stack([row_even, row_odd], axis=-3)
    order = 2 * same_part.shape[-1]
    gram = whole.reshape(same_part.shape[:-2] + (order, order))
    return gram + noise[..., None, None] * jnp.eye(order, dtype=jnp.float32)


def estimate_transmitted(cholesky_triangle, whitened_observation, retained_branches):
    terminal_number = cholesky_triangle.shape[-1] // 2
    outer_dimensions = retained_branches.shape[:-1]
    kept_branch_number = retained_branches.shape[-1] // terminal_number
    constellation_position = retained_branches.reshape(
        outer_dimensions + (kept_branch_number, terminal_number)
    )
    inphase_amplitude = (2 * (constellation_position % 8) - 7).astype(jnp.float32)
    quadrature_amplitude = (2 * (constellation_position // 8) - 7).astype(jnp.float32)
    branch_vector = (
        jnp.stack([inphase_amplitude, quadrature_amplitude], axis=-1).reshape(
            outer_dimensions + (kept_branch_number, 2 * terminal_number)
        )
        * constellation_norm
    )
    upper_factor = jnp.swapaxes(cholesky_triangle, -1, -2)
    mapped = jnp.einsum(
        "bsij,bstkj->bstki", upper_factor, branch_vector, precision=lax.Precision.HIGHEST
    )
    remainder_error = jnp.swapaxes(whitened_observation, -1, -2)[..., None, :] - mapped
    squared_errors = (
        (remainder_error * remainder_error)
        .reshape(outer_dimensions + (kept_branch_number, terminal_number, 2))
        .sum(axis=-1)
    )
    accrued_metric = jnp.cumsum(squared_errors[..., ::-1], axis=-1)[..., ::-1] / terminal_number
    return accrued_metric.reshape(outer_dimensions + (kept_branch_number * terminal_number,))


def add_tree(earlier, later):
    return jax.tree.map(jnp.add, earlier, later)


def flatten_last(array_in):
    return array_in.reshape(array_in.shape[:2] + (-1,))


def local(propagation_gains, observed_samples, disturbance_variance, retained_branches):
    terminal_number = propagation_gains.shape[2] // 2
    sym_total = observed_samples.shape[2] // 2
    clusters = lax.axis_size("chain")
    sub_share = propagation_gains.shape[1] // clusters
    raw_gram = jnp.einsum(
        "bsra,bsqa->bsrq", propagation_gains, propagation_gains, preferred_element_type=jnp.float32
    )
    raw_cross = jnp.einsum(
        "bsra,bsqa->bsrq", propagation_gains, observed_samples, preferred_element_type=jnp.float32
    )
    statistic = (flatten_last(raw_gram), flatten_last(raw_cross))
    zeros_tree = jax.tree.map(jnp.zeros_like, statistic)
    earlier = prefix(statistic, "chain", add_tree, zeros_tree)
    running = add_tree(earlier, statistic)
    totals = jax.tree.map(lambda part: from_root(part, "chain", clusters - 1), running)
    start = lax.axis_index("chain") * sub_share
    shares = jax.tree.map(
        lambda whole: lax.dynamic_slice_in_dim(whole, start, sub_share, 1), totals
    )
    outer_dimensions = (1, sub_share)
    same_part, cross_part, rhs = fold_stats(
        shares[0].reshape(outer_dimensions + (2 * terminal_number, 2 * terminal_number)),
        shares[1].reshape(outer_dimensions + (2 * terminal_number, 2 * sym_total)),
    )
    band_index = lax.axis_index("par")
    own_noise = lax.dynamic_slice_in_dim(disturbance_variance, band_index, 1, 0)
    lower_own = jnp.linalg.cholesky(assemble(same_part, cross_part, own_noise))
    rotated_own = jax.scipy.linalg.solve_triangular(lower_own, rhs, lower=True)
    cholesky_triangle = lax.all_gather(lower_own, "par", axis=0, tiled=True)
    whitened_observation = lax.all_to_all(
        rotated_own, "par", split_axis=3, concat_axis=0, tiled=True
    )
    return estimate_transmitted(cholesky_triangle, whitened_observation, retained_branches)


def solution(mesh):
    placed = (
        P("par", None, None, "chain"),
        P("par", None, None, "chain"),
        P(None, "chain"),
        P(None, "chain", "par", None),
    )
    return jax.shard_map(
        local, mesh=mesh, in_specs=placed, out_specs=P(None, "chain", "par", None), check_vma=False
    )
```

profile of v0, /device:TPU:0, one launch (start us, length us, event | category | flops | bytes accessed | tf_op | source)
XLA Modules:
  0.0 226.0 jit_solution(8765339987140583563)
XLA Ops:
  6.5 1.6 copy-done
  8.1 1.9 fusion
  15.1 1.1 reshape.317
  17.0 1.3 copy.136
  18.5 18.7 %all-gather.5.cloned.1.call-done = f32[8,1,16,2048]{3,2,1,0:T(8,128)} async-done(((f32[1,1,16,2048]{3,2,1,0:T(8,128)}), f32[8,1,16,2048]{3,2,1,0:T(8,128)}) %all-gather.5.cloned.1.call-update) | async-done | bytes 1048592 | tf_op jit(solution)/shard_map/all_gather | solution.py:11
  37.2 29.7 %all-gather.3.cloned.1.call-done = f32[8,1,16,4096]{3,2,1,0:T(8,128)} async-done(((f32[1,1,16,4096]{3,2,1,0:T(8,128)}), f32[8,1,16,4096]{3,2,1,0:T(8,128)}) %all-gather.3.cloned.1.call-update) | async-done | bytes 2097168 | tf_op jit(solution)/shard_map/all_gather | solution.py:11
  66.9 16.1 %while.16 = (s32[]{:T(128)}, f32[1,16,4096]{2,1,0:T(8,128)S(1)}, f32[1,16,2048]{2,1,0:T(8,128)S(1)}, s32[]{:T(128)}, f32[8,1,16,4096]{3,2,1,0:T(8,128)}, /*index=5*/f32[8,1,16,2048]{3,2,1,0:T(8,128)}, s32[]{:T(128)}, s32[]{:T(128)}) while((s32[]{:T(128)}, f32[1,16,4096]{2,1,0:T(8,128)S(1)}, f32[1,16,2048]{2,1,0:T(8,128)S(1)}, ...), condition=%wide.region_1.2_spmd.clone, body=%wide.region_0.1_spmd.clone.sunk | while | flops 294916 | bytes 1179771 | solution.py:21
  67.9 1.0 add_select_fusion.8
  69.9 1.0 add_select_fusion.8
  71.9 1.0 add_select_fusion.8
  73.9 1.0 add_select_fusion.8
  76.0 1.0 add_select_fusion.8
  78.0 1.0 add_select_fusion.8
  80.0 1.0 add_select_fusion.8
  84.5 54.6 %all-reduce.3.cloned.1.call-done = (f32[1,16,4096]{2,1,0:T(8,128)}, f32[1,16,2048]{2,1,0:T(8,128)}) async-done(((f32[1,16,4096]{2,1,0:T(8,128)}, f32[1,16,2048]{2,1,0:T(8,128)}), (f32[1,16,4096]{2,1,0:T(8,128)}, f32[1,16,2048]{2,1,0:T(8,128)})) %all-reduce.3.cloned.1.call-update) | async-done | bytes 393232 | tf_op jit(solution)/shard_map/psum | solution.py:26
  141.9 1.3 slice_add_fusion.1
  143.3 1.3 copy.129
  144.6 1.3 copy.130
  146.0 3.5 %reshape_reshape.6 = f32[1,2,32,2,32,2]{5,4,3,2,1,0:T(8,128)} reshape(f32[1,2,4096]{2,1,0:T(2,128)S(1)} %constant_dynamic-slice_fusion.1) | data formatting | bytes 65536 | tf_op jit(solution)/shard_map/reshape;reshape | solution.py:32
  149.5 3.4 %fusion.5 = (f32[2,32,32]{2,1,0:T(8,128)S(1)}, f32[2,32,32]{2,1,0:T(8,128)S(1)}) fusion(f32[1,2,32,2,32,2]{5,4,3,2,1,0:T(8,128)} %reshape_reshape.6), kind=kLoop, calls=%fused_computation.10 | loop fusion | flops 4096 | bytes 49152 | tf_op jit(solution)/shard_map/sub | solution.py:34
  153.0 3.0 %copy.146 = f32[1,2,32,2,32,2]{3,2,5,4,1,0:T(8,128)} copy(f32[1,2,32,2,32,2]{4,2,1,5,3,0:T(8,128)S(1)} %pad_maximum_fusion) | data formatting | bytes 65536 | tf_op jit(solution)/shard_map/reshape | solution.py:49
  156.0 3.3 %reshape.321 = f32[1,2,64,64]{2,3,1,0:T(8,128)S(1)} reshape(f32[1,2,32,2,32,2]{3,2,5,4,1,0:T(8,128)} %copy.146) | data formatting | bytes 65536 | tf_op jit(solution)/shard_map/reshape | solution.py:49
  159.5 11.7 %custom-call.8 = f32[1,2,64,64]{3,2,1,0:T(8,128)S(1)} custom-call(f32[1,2,64,64]{3,2,1,0:T(8,128)S(1)} %fusion.18), custom_call_target="Cholesky" | custom-call | tf_op jit(solution)/shard_map/jit(cholesky)/cholesky | solution.py:117
  171.5 9.8 %custom-call.9 = f32[2,1,64,64]{2,3,1,0:T(8,128)S(1)} custom-call(f32[2,1,64,64]{3,2,1,0:T(8,128)S(1)} %get-tuple-element.154), custom_call_target="InvertDiagBlocksLowerTriangular" | custom-call | tf_op jit(solution)/shard_map/jit(_solve_triangular)/vmap()/triangular_solve | solution.py:118
  182.3 4.5 %all-to-all-start = ((f32[4,1,512]{2,1,0:T(1,128)}), f32[4,1,512]{2,1,0:T(1,128)S(1)}, u32[]{:S(2)}, u32[]{:S(2)}) async-start(f32[4,1,512]{2,1,0:T(1,128)} %reshape.325), calls=%async_computation | async-start | bytes 16384 | tf_op jit(solution)/shard_map/all_to_all | solution.py:120
  186.8 14.5 %all_gather.11 = f32[4,2,64,64]{3,2,1,0:T(8,128)S(1)} all-gather(f32[1,2,64,64]{3,2,1,0:T(8,128)S(1)} %get-tuple-element.155), channel_id=1, replica_groups=mesh['chain'=8,'par'=4] {'par'}, dimensions={0}, use_global_device_ids=true | all-gather | bytes 163840 | tf_op jit(solution)/shard_map/all_gather | solution.py:119
  202.7 2.6 %fusion.4 = f32[4,2,4,32,64]{4,3,2,1,0:T(8,128)} fusion(f32[4,2,4,32,64]{3,4,2,1,0:T(8,128)S(1)} %bitcast.64, f32[4,2,64,64]{3,2,1,0:T(8,128)S(1)} %all_gather.11, f32[4,2,4,64]{3,2,1,0:T(4,128)S(1)} %bitcast.69), kind=kOutput, calls=%fused_computation.7 | convolution fusion | flops 50462720 | bytes 663552 | tf_op jit(solution)/shard_map/bsij,bstkj->bstki/dot_general | solution.py:69
  205.3 1.4 copy.138
  206.7 2.3 %reduce_sum.9 = f32[4,2,4,32,32]{3,4,2,1,0:T(8,128)} reduce(f32[4,2,4,32,32,2]{3,5,4,2,1,0:T(2,128)S(1)} %bitcast.65, f32[]{:T(128)} %constant.116.clone.1), dimensions={5}, to_apply=%region_6.7 | reduce | flops 32768 | bytes 393220 | tf_op jit(solution)/shard_map/reduce_sum | solution.py:76
  209.0 1.1 rev.6
  210.3 6.1 %reduce_window_sum.11 = f32[4,2,4,32,32]{4,3,2,1,0:T(8,128)S(1)} reduce-window(f32[4,2,4,32,32]{4,3,2,1,0:T(8,128)S(1)} %copy.139, f32[]{:T(128)} %constant.116.clone.1), window={size=1x1x1x1x32 pad=0_0x0_0x0_0x0_0x31_0}, to_apply=%region_7.8 | reduce-window | flops 1015808 | bytes 262148 | tf_op jit(solution)/shard_map/jit(cumsum)/reduce_window_sum | solution.py:78
  217.4 1.1 broadcast_multiply_fusion
  (67 shorter events, 23.8 us)
Async XLA Ops:
  6.5 1.6 copy-start
  6.5 30.7 %all-gather.5.cloned.1.call-start = ((), (), s32[]{:S(2)}) async-start(), calls=%async_computation.2 | async-start | bytes 1179648 | tf_op jit(solution)/shard_map/all_gather | solution.py:11
  11.0 55.9 %all-gather.3.cloned.1.call-start = ((), (), s32[]{:S(2)}) async-start(), calls=%async_computation.1 | async-start | bytes 2359296 | tf_op jit(solution)/shard_map/all_gather | solution.py:11
  12.6 126.5 %all-reduce.3.cloned.1.call-start = ((), (), s32[]{:S(2)}) async-start(), calls=%async_computation.3 | async-start | bytes 786432 | tf_op jit(solution)/shard_map/psum | solution.py:26
  16.8 1.5 copy-start.5
  66.9 16.1 %copy-start.3 = (f32[1,16,2048]{2,1,0:T(8,128)S(1)}, f32[1,16,2048]{2,1,0:T(8,128)}, u32[]{:S(2)}) copy-start(f32[1,16,2048]{2,1,0:T(8,128)} %reshape.316) | copy-start | bytes 393220
  66.9 16.8 %copy-start.2 = (f32[1,16,4096]{2,1,0:T(8,128)S(1)}, f32[1,16,4096]{2,1,0:T(8,128)}, u32[]{:S(2)}) copy-start(f32[1,16,4096]{2,1,0:T(8,128)} %reshape.314) | copy-start | bytes 786436
  153.0 6.3 %copy-start.4 = (f32[64,64]{0,1:T(8,128)S(1)}, f32[64,64]{0,1:T(8,128)}, u32[]{:S(2)}) copy-start(f32[64,64]{0,1:T(8,128)} %copy.125) | copy-start | bytes 49156
  156.0 46.7 %copy-start.1 = (f32[4,2,4,32,32,2]{3,5,4,2,1,0:T(2,128)S(1)}, f32[4,2,4,32,32,2]{3,5,4,2,1,0:T(2,128)}, u32[]{:S(2)}) copy-start(f32[4,2,4,32,32,2]{3,5,4,2,1,0:T(2,128)} %copy.136) | copy-start | bytes 786436
  182.3 19.1 %all-to-all-start = ((f32[4,1,512]{2,1,0:T(1,128)}), f32[4,1,512]{2,1,0:T(1,128)S(1)}, u32[]{:S(2)}, u32[]{:S(2)}) async-start(f32[4,1,512]{2,1,0:T(1,128)} %reshape.325), calls=%async_computation | async-start | bytes 16384 | tf_op jit(solution)/shard_map/all_to_all | solution.py:120
Sparse Core Ops, SparseCore 0:
  11.1 26.0 all-gather.4
  39.1 27.7 all-gather.2
  84.6 54.4 all-reduce.2
where the time goes:
time: 227 us; the launch traced here: 226 us
  waiting for transfers between devices  103 us (45%)
  other arithmetic  55 us (24%)
  local copies, waits for them, and re-layouts  29.7 us (13%)
  blocking collectives  14.5 us (6%)
  between operations  13.3 us (6%)
  matrix products  5.48 us (2%)
  starting transfers between devices  4.62 us (2%)
    psum x1, waiting for transfers between devices, from_root(): return lax.psum(block, axis)  54.6 us
    all_gather x2, waiting for transfers between devices, prefix(): everything = jax.tree.map(lambda part: lax.all_gather(part, axis), x)  48.4 us
    select_n x16, other arithmetic, turn(): return jax.tree.map(lambda a, b: jnp.where(reached, a, b), new, before)  15.9 us
    all_gather x1, blocking collectives, local(): cholesky_triangle = lax.all_gather(lower_own, 'par', axis=0, tiled=True)  14.5 us
    another operation x4, other arithmetic, local(): lower_own = jnp.linalg.cholesky(assemble(same_part, cross_part, own_noise))  11.9 us
    another operation x3, other arithmetic, local(): rotated_own = jax.scipy.linalg.solve_triangular(lower_own, rhs, lower=True)  9.93 us
    reshape x2, local copies, waits for them, and re-layouts, assemble(): gram = whole.reshape(same_part.shape[:-2] + (order, order))  6.26 us
    another operation x1, other arithmetic, estimate_transmitted(): jnp.cumsum(squared_errors[..., ::-1], axis=-1)[..., ::-1] / terminal_number  6.14 us
  transfers between devices with their start and end apart: 4, of which 3 were waited for; matrix products, arithmetic and copies ran while one was open for 3% of the time, Pallas kernels for 0%

commit v1 on v0

v1 whole, which is shorter than its diff:
```python
import functools
import jax
import jax.numpy as jnp
from jax import lax
from jax.experimental import pallas as pl
from jax.experimental.pallas import tpu as pltpu
from jax.sharding import PartitionSpec as P

constellation_norm = 1.0 / 42.0**0.5
LANES = 128
MESH = pl.DeviceIdType.MESH
NT = (((1,), (1,)), ((), ()))


def iota(shape, dim):
    return lax.broadcasted_iota(jnp.int32, shape, dim)


def split(x):
    high = x.astype(jnp.bfloat16)
    return high, (x - high.astype(jnp.float32)).astype(jnp.bfloat16)


def pair_swap(x):
    even = iota(x.shape, 1) % 2 == 0
    return jnp.where(even, pltpu.roll(x, LANES - 1, 1), pltpu.roll(x, 1, 1))


def eliminate(mats, users):
    groups = users // 8
    blocks, turned = [], []
    for mat in mats:
        odd = iota((8, LANES), 1) % 2 == 1
        parts = [mat[8 * g : 8 * g + 8, :] for g in range(groups)]
        blocks.append(parts)
        turned.append([jnp.where(odd, pair_swap(p), -pair_swap(p)) for p in parts])
    row = iota((8, LANES), 0)
    for j in range(users - 1):
        home, at = divmod(j, 8)
        for a, ia in zip(blocks, turned):
            pivot_row, turned_row = a[home][at : at + 1, :], ia[home][at : at + 1, :]
            inverse = 1.0 / pivot_row[:, 2 * j : 2 * j + 1]
            pivot_row, turned_row = pivot_row * inverse, turned_row * inverse
            for g in range(home + (at == 7), groups):
                real = jnp.broadcast_to(a[g][:, 2 * j : 2 * j + 1], (8, LANES))
                imag = jnp.broadcast_to(a[g][:, 2 * j + 1 : 2 * j + 2], (8, LANES))
                if g == home:
                    real = jnp.where(row > at, real, 0.0)
                    imag = jnp.where(row > at, imag, 0.0)
                a[g] = a[g] - (real * pivot_row + imag * turned_row)
                ia[g] = ia[g] - (real * turned_row - imag * pivot_row)
    lane, line = iota((users, LANES), 1), iota((users, LANES), 0)
    keep = (lane >= 2 * line) & (lane != 2 * line + 1) | (lane >= 2 * users)
    out = []
    for a in blocks:
        full = jnp.concatenate(a, axis=0)
        pivots = jnp.sum(jnp.where(lane == 2 * line, full, 0.0), axis=1, keepdims=True)
        out.append(jnp.where(keep, full * lax.rsqrt(pivots), 0.0))
    return out


def kernel(
    dims, noise_ref, gains_ref, samples_ref, branches_ref, out_ref,
    held, raw, part, came, points, packed, taken, rotations,
    load_sem, send_sem, recv_sem, usend_sem, urecv_sem,
):
    clusters, bands, users, symbols, share, mine_t, pieces = dims
    copies = LANES // users
    lines = pieces * mine_t
    me, band = lax.axis_index("chain"), lax.axis_index("par")

    barrier = pltpu.get_barrier_semaphore()
    for k in range(1, clusters):
        pl.semaphore_signal(barrier, inc=1, device_id={"chain": lax.rem(me + k, clusters)}, device_id_type=MESH)
    for k in range(1, bands):
        pl.semaphore_signal(barrier, inc=1, device_id={"par": lax.rem(band + k, bands)}, device_id_type=MESH)

    order = list(range(1, clusters)) + [0]
    loads = {}
    for k in order:
        tones = pl.ds(lax.rem(me + k, clusters) * share, share)
        loads[k] = (
            pltpu.make_async_copy(
                gains_ref.at[0, tones], held.at[k, :, pl.ds(0, 2 * users)], load_sem.at[0, k]
            ),
            pltpu.make_async_copy(
                samples_ref.at[0, tones], held.at[k, :, pl.ds(2 * users, 2 * symbols)], load_sem.at[1, k]
            ),
        )
        for copy in loads[k]:
            copy.start()

    raw[...] = jnp.zeros_like(raw)
    even = iota((users, LANES), 1) % 2 == 0
    sends = []
    for number, k in enumerate(order):
        for copy in loads[k]:
            copy.wait()
        for s in range(share):
            slot = (number * share + s) % raw.shape[0]
            both = held[k, s]
            raw[slot, :, : 2 * (users + symbols)] = lax.dot_general(
                both[: 2 * users], both, NT, preferred_element_type=jnp.float32
            )
            on_even = raw[slot, pl.ds(0, users, stride=2), :]
            on_odd = raw[slot, pl.ds(1, users, stride=2), :]
            part[k, s] = pair_swap(on_odd) + jnp.where(even, on_even, -on_even)
        if k:
            if number == 0:
                pl.semaphore_wait(barrier, clusters + bands - 2)
            copy = pltpu.make_async_remote_copy(
                src_ref=part.at[k], dst_ref=came.at[k], send_sem=send_sem.at[k], recv_sem=recv_sem.at[k],
                device_id={"chain": lax.rem(me + k, clusters)}, device_id_type=MESH,
            )
            copy.start()
            sends.append(copy)

    for b in range(bands):
        for s in range(share):
            q = jnp.concatenate(
                [branches_ref[b, s, :, LANES * r : LANES * (r + 1)] for r in range(pieces)], axis=0
            )
            points[b, s, :, :LANES] = (2 * (q & 7) - 7).astype(jnp.float32).astype(jnp.bfloat16)
            points[b, s, :, LANES:] = (2 * (q >> 3) - 7).astype(jnp.float32).astype(jnp.bfloat16)

    lane, line = iota((users, LANES), 1), iota((users, LANES), 0)
    totals = [part[0, s] for s in range(share)]
    for copy in sends:
        copy.wait_recv()
    for k in range(1, clusters):
        totals = [total + came[k, s] for s, total in enumerate(totals)]
    mats = [
        jnp.where(lane == 2 * line, total + noise_ref[band, s], total) for s, total in enumerate(totals)
    ]
    factors = eliminate(mats, users)

    source, target = iota((LANES, LANES), 0), iota((LANES, LANES), 1) % (2 * users)
    spread = (source == 2 * (target % users) + target // users).astype(jnp.float32).astype(jnp.bfloat16)
    rows = 2 * mine_t
    r, c = iota((bands * rows, LANES), 0), iota((bands * rows, LANES), 1)
    is_odd = (r % rows) // mine_t
    wanted = 2 * users + 2 * ((r // rows) * mine_t + r % mine_t) + is_odd
    pick = jnp.where(c == wanted, (1 - 2 * is_odd).astype(jnp.float32), 0.0).astype(jnp.bfloat16)
    pick = jnp.concatenate([pick, pick], axis=1)
    half = users // 2
    left = iota((half, LANES), 1) < 2 * users
    for s, factor in enumerate(factors):
        high, low = split(factor * constellation_norm)
        wide = jnp.dot(high, spread, preferred_element_type=jnp.float32) + jnp.dot(
            low, spread, preferred_element_type=jnp.float32
        )
        folded = jnp.where(left, wide[:half], wide[half:])
        for k in range(bands):
            packed[k, s, :half] = folded
        high, low = split(factor)
        weights = jnp.concatenate(
            [jnp.concatenate([high] * copies, axis=0), jnp.concatenate([low] * copies, axis=0)], axis=1
        )
        rotations[s] = lax.dot_general(pick, weights, NT, preferred_element_type=jnp.float32)
        for k in range(bands):
            peer = lax.rem(band + k, bands)
            packed[k, s, half:] = rotations[s, pl.ds(pl.multiple_of(peer * rows, rows), rows), :]
    usends = []
    for k in range(1, bands):
        copy = pltpu.make_async_remote_copy(
            src_ref=packed.at[k], dst_ref=taken.at[k], send_sem=usend_sem.at[k], recv_sem=urecv_sem.at[k],
            device_id={"par": lax.rem(band + k, bands)}, device_id_type=MESH,
        )
        copy.start()
        usends.append(copy)

    sr, sc = iota((LANES, LANES), 0), iota((LANES, LANES), 1)
    suffix = jnp.where((sr // users == sc // users) & (sr >= sc), 1.0 / users, 0.0).astype(jnp.bfloat16)
    suffix = jnp.concatenate([suffix, suffix], axis=0)
    lane_block = lane // users
    for k in range(bands):
        if k:
            usends[k - 1].wait_recv()
        b = lax.rem(band + bands - k, bands)
        box = taken if k else packed
        for s in range(share):
            folded = box[k, s, :half]
            crossed = pltpu.roll(folded, 2 * users, 1)
            first = jnp.concatenate(
                [jnp.where(left, folded, crossed), jnp.where(left, crossed, folded)], axis=0
            )
            second = pltpu.roll(first, users, 1)
            ons, offs = [], []
            for i in range(copies):
                here = lane_block == i
                real, imag = (first, second) if i % 2 == 0 else (second, first)
                real, imag = jnp.where(here, real, 0.0), jnp.where(here, imag, 0.0)
                ons.append(jnp.concatenate([real, imag], axis=1))
                offs.append(jnp.concatenate([-imag, real], axis=1))
            high, low = split(jnp.concatenate(ons + offs, axis=0))
            p = points[b, s]
            mapped = lax.dot_general(p, high, NT, preferred_element_type=jnp.float32) + lax.dot_general(
                p, low, NT, preferred_element_type=jnp.float32
            )
            on = jnp.concatenate([box[k, s, half : half + mine_t]] * pieces, axis=0) - mapped[:, :LANES]
            off = jnp.concatenate([box[k, s, half + mine_t :]] * pieces, axis=0) - mapped[:, LANES:]
            high, low = split(on * on + off * off)
            result = jnp.dot(
                jnp.concatenate([high, low], axis=1), suffix, preferred_element_type=jnp.float32
            )
            for r in range(pieces):
                out_ref[b, s, :, LANES * r : LANES * (r + 1)] = result[mine_t * r : mine_t * (r + 1)]
    for copy in sends + usends:
        copy.wait_send()


def local(propagation_gains, observed_samples, disturbance_variance, retained_branches):
    clusters, bands = lax.axis_size("chain"), lax.axis_size("par")
    _, tones, double_users, antennas = propagation_gains.shape
    users, symbols = double_users // 2, observed_samples.shape[2] // 2
    share, mine_t = tones // clusters, symbols // bands
    pieces = retained_branches.shape[-1] // LANES
    dims = (clusters, bands, users, symbols, share, mine_t, pieces)
    f32, bf16 = jnp.float32, jnp.bfloat16
    vmem, dma = pltpu.VMEM, pltpu.SemaphoreType.DMA
    payload = users // 2 + 2 * mine_t
    return pl.pallas_call(
        functools.partial(kernel, dims),
        out_shape=jax.ShapeDtypeStruct(retained_branches.shape, f32),
        in_specs=[
            pl.BlockSpec(memory_space=pltpu.SMEM),
            pl.BlockSpec(memory_space=pl.ANY),
            pl.BlockSpec(memory_space=pl.ANY),
            pl.BlockSpec(memory_space=pltpu.VMEM),
        ],
        out_specs=pl.BlockSpec(memory_space=pltpu.VMEM),
        scratch_shapes=[
            vmem((clusters, share, 2 * (users + symbols), antennas), bf16),
            vmem((4, 2 * users, LANES), f32),
            vmem((clusters, share, users, LANES), f32),
            vmem((clusters, share, users, LANES), f32),
            vmem((bands, share, pieces * mine_t, 2 * LANES), bf16),
            vmem((bands, share, payload, LANES), f32),
            vmem((bands, share, payload, LANES), f32),
            vmem((share, bands * 2 * mine_t, LANES), f32),
            dma((2, clusters)), dma((clusters,)), dma((clusters,)), dma((bands,)), dma((bands,)),
        ],
        compiler_params=pltpu.CompilerParams(collective_id=0, has_side_effects=True),
        name="detect",
    )(disturbance_variance, propagation_gains, observed_samples, retained_branches)


def solution(mesh):
    placed = (
        P("par", None, None, "chain"),
        P("par", None, None, "chain"),
        P(None, "chain"),
        P(None, "chain", "par", None),
    )
    return jax.shard_map(
        local, mesh=mesh, in_specs=placed, out_specs=P(None, "chain", "par", None), check_vma=False
    )
```

time: 227 us -> 24.4 us (0.11)
  waiting for transfers between devices: 103 us -> 0 us
  other arithmetic: 55 us -> 0 us
  local copies, waits for them, and re-layouts: 29.7 us -> 2.9 us
  Pallas kernels: 0 us -> 21.3 us
  blocking collectives: 14.5 us -> 0 us
  between operations: 13.3 us -> 0.01 us
  matrix products: 5.48 us -> 0 us
  starting transfers between devices: 4.62 us -> 0 us
    psum x1 -> x0, waiting for transfers between devices: 54.6 us -> none  [from_root(): return lax.psum(block, axis)]
    all_gather x2 -> x0, waiting for transfers between devices: 48.4 us -> none  [prefix(): everything = jax.tree.map(lambda part: lax.all_gather(part, axis), x)]
    another operation x11 -> x0, other arithmetic: 28 us -> none  [the longest x4 11.9 us: local(): lower_own = jnp.linalg.cholesky(assemble(same_part, cross_part, own_noise))]
    pallas_call x0 -> x1, Pallas kernels: none -> 21.3 us  [local(): pl.pallas_call(functools.partial(kernel, dims), out_shape=jax.ShapeDtypeS...]
    select_n x18 -> x0, other arithmetic: 17.3 us -> none  [the longest x16 15.9 us: turn(): return jax.tree.map(lambda a, b: jnp.where(reached, a, b), new, before)]
    all_gather x1 -> x0, blocking collectives: 14.5 us -> none  [local(): cholesky_triangle = lax.all_gather(lower_own, 'par', axis=0, tiled=True)]
    reshape x6 -> x0, local copies, waits for them, and re-layouts: 10 us -> none  [the longest x2 6.26 us: assemble(): gram = whole.reshape(same_part.shape[:-2] + (order, order))]
    another operation x5 -> x0, local copies, waits for them, and re-layouts: 6.39 us -> none  [the longest x1 3.52 us: fold_stats(): raw_gram.reshape(outer_dimensions + (terminal_number, 2, terminal_number,...]
  transfers between devices with their start and end apart: 4 -> 0, of which waited for: 3 -> 0; matrix products, arithmetic and copies ran while one was open for 3% -> 0% of each run, Pallas kernels for 0% -> 0%
where the time goes in v1:
time: 24.4 us; the launch traced here: 24.3 us
  Pallas kernels  21.3 us (87%)
  local copies, waits for them, and re-layouts  2.9 us (12%)
    pallas_call x1, Pallas kernels, local(): pl.pallas_call(functools.partial(kernel, dims), out_shape=jax.ShapeDtypeS...  21.3 us
    unnamed x2, local copies, waits for them, and re-layouts  2.9 us

profile of v1, /device:TPU:0, one launch (start us, length us, event | category | flops | bytes accessed | tf_op | source)
XLA Modules:
  0.0 24.3 jit_solution(17648569132550471376)
XLA Ops:
  0.0 1.3 %copy.5.noise_ref = f32[4,2]{1,0:T(4,128)} copy(f32[4,2]{0,1:T(2,128)} %param.6) | data formatting | bytes 64 | tf_op args[2]
  1.3 21.3 %detect.1 = f32[4,2,4,1024]{3,2,1,0:T(4,128)} custom-call(f32[4,2]{1,0:T(4,128)} %copy.5.noise_ref, bf16[1,16,64,1024]{3,2,1,0:T(8,128)(2,1)} %gains_ref.1, bf16[1,16,32,1024]{3,2,1,0:T(8,128)(2,1)} %samples_ref.1, s32[4,2,4,1024]{3,2,1,0:T(4,128)} %branches_ref.1), custom_call_target="tpu_custom_call" | custom-call | tf_op jit(solution)/shard_map/detect/pallas_call | solution.py:222
  22.7 1.6 %copy.7 = f32[4,2,4,1024]{3,2,1,0:T(4,128)} copy(f32[4,2,4,1024]{3,2,1,0:T(4,128)} %detect.1) | data formatting | bytes 262144

commit v2 on v1

--- a/solution.py
+++ b/solution.py
@@ -8,6 +8,7 @@
 
 constellation_norm = 1.0 / 42.0**0.5
 LANES = 128
+PANEL = 4
 MESH = pl.DeviceIdType.MESH
 NT = (((1,), (1,)), ((), ()))
 
@@ -35,20 +36,35 @@
         blocks.append(parts)
         turned.append([jnp.where(odd, pair_swap(p), -pair_swap(p)) for p in parts])
     row = iota((8, LANES), 0)
-    for j in range(users - 1):
-        home, at = divmod(j, 8)
-        for a, ia in zip(blocks, turned):
-            pivot_row, turned_row = a[home][at : at + 1, :], ia[home][at : at + 1, :]
-            inverse = 1.0 / pivot_row[:, 2 * j : 2 * j + 1]
-            pivot_row, turned_row = pivot_row * inverse, turned_row * inverse
-            for g in range(home + (at == 7), groups):
-                real = jnp.broadcast_to(a[g][:, 2 * j : 2 * j + 1], (8, LANES))
-                imag = jnp.broadcast_to(a[g][:, 2 * j + 1 : 2 * j + 2], (8, LANES))
-                if g == home:
-                    real = jnp.where(row > at, real, 0.0)
-                    imag = jnp.where(row > at, imag, 0.0)
-                a[g] = a[g] - (real * pivot_row + imag * turned_row)
-                ia[g] = ia[g] - (real * turned_row - imag * pivot_row)
+    for start in range(0, users, PANEL):
+        home = start // 8
+        panels = [
+            [
+                {g: jnp.broadcast_to(a[g][:, lane : lane + 1], (8, LANES)) for g in range(home, groups)}
+                for lane in range(2 * start, 2 * (start + PANEL))
+            ]
+            for a in blocks
+        ]
+        for j in range(start, min(start + PANEL, users - 1)):
+            at, c = j % 8, j - start
+            for a, ia, panel in zip(blocks, turned, panels):
+                real, imag = panel[2 * c], panel[2 * c + 1]
+                inverse = 1.0 / real[home][at : at + 1, :]
+                pivot_row = a[home][at : at + 1, :] * inverse
+                turned_row = ia[home][at : at + 1, :] * inverse
+                later = [
+                    (d, real[home][at + d - c : at + d - c + 1, :] * inverse, imag[home][at + d - c : at + d - c + 1, :] * inverse)
+                    for d in range(c + 1, PANEL)
+                ]
+                for g in range(home + (at == 7), groups):
+                    fr, fi = real[g], imag[g]
+                    if g == home:
+                        fr, fi = jnp.where(row > at, fr, 0.0), jnp.where(row > at, fi, 0.0)
+                    for d, x, y in later:
+                        panel[2 * d][g] = panel[2 * d][g] - (fr * x + fi * y)
+                        panel[2 * d + 1][g] = panel[2 * d + 1][g] - (fi * x - fr * y)
+                    a[g] = a[g] - (fr * pivot_row + fi * turned_row)
+                    ia[g] = ia[g] - (fr * turned_row - fi * pivot_row)
     lane, line = iota((users, LANES), 1), iota((users, LANES), 0)
     keep = (lane >= 2 * line) & (lane != 2 * line + 1) | (lane >= 2 * users)
     out = []
@@ -60,9 +76,9 @@
 
 
 def kernel(
-    dims, noise_ref, gains_ref, samples_ref, branches_ref, out_ref,
-    held, raw, part, came, points, packed, taken, rotations,
-    load_sem, send_sem, recv_sem, usend_sem, urecv_sem,
+    dims, noise_any, gains_ref, samples_ref, branches_any, out_ref,
+    noise_ref, branches_ref, held, raw, part, came, points, packed, taken, rotations,
+    small_sem, load_sem, send_sem, recv_sem, usend_sem, urecv_sem,
 ):
     clusters, bands, users, symbols, share, mine_t, pieces = dims
     copies = LANES // users
@@ -90,6 +106,12 @@
         for copy in loads[k]:
             copy.start()
 
+    small = (
+        pltpu.make_async_copy(noise_any, noise_ref, small_sem.at[0]),
+        pltpu.make_async_copy(branches_any, branches_ref, small_sem.at[1]),
+    )
+    for copy in small:
+        copy.start()
     raw[...] = jnp.zeros_like(raw)
     even = iota((users, LANES), 1) % 2 == 0
     sends = []
@@ -115,6 +137,8 @@
             copy.start()
             sends.append(copy)
 
+    for copy in small:
+        copy.wait()
     for b in range(bands):
         for s in range(share):
             q = jnp.concatenate(
@@ -124,13 +148,17 @@
             points[b, s, :, LANES:] = (2 * (q >> 3) - 7).astype(jnp.float32).astype(jnp.bfloat16)
 
     lane, line = iota((users, LANES), 1), iota((users, LANES), 0)
+    noises = [
+        jnp.sum(jnp.where(iota((1, bands), 1) == band, noise_ref[s : s + 1, :], 0.0), axis=1, keepdims=True)
+        for s in range(share)
+    ]
     totals = [part[0, s] for s in range(share)]
     for copy in sends:
         copy.wait_recv()
     for k in range(1, clusters):
         totals = [total + came[k, s] for s, total in enumerate(totals)]
     mats = [
-        jnp.where(lane == 2 * line, total + noise_ref[band, s], total) for s, total in enumerate(totals)
+        jnp.where(lane == 2 * line, total + noises[s], total) for s, total in enumerate(totals)
     ]
     factors = eliminate(mats, users)
 
@@ -223,13 +251,15 @@
         functools.partial(kernel, dims),
         out_shape=jax.ShapeDtypeStruct(retained_branches.shape, f32),
         in_specs=[
-            pl.BlockSpec(memory_space=pltpu.SMEM),
-            pl.BlockSpec(memory_space=pl.ANY),
-            pl.BlockSpec(memory_space=pl.ANY),
-            pl.BlockSpec(memory_space=pltpu.VMEM),
+            pl.BlockSpec(memory_space=pl.ANY),
+            pl.BlockSpec(memory_space=pl.ANY),
+            pl.BlockSpec(memory_space=pl.ANY),
+            pl.BlockSpec(memory_space=pl.ANY),
         ],
         out_specs=pl.BlockSpec(memory_space=pltpu.VMEM),
         scratch_shapes=[
+            vmem(disturbance_variance.shape[::-1], f32),
+            vmem(retained_branches.shape, jnp.int32),
             vmem((clusters, share, 2 * (users + symbols), antennas), bf16),
             vmem((4, 2 * users, LANES), f32),
             vmem((clusters, share, users, LANES), f32),
@@ -238,11 +268,11 @@
             vmem((bands, share, payload, LANES), f32),
             vmem((bands, share, payload, LANES), f32),
             vmem((share, bands * 2 * mine_t, LANES), f32),
-            dma((2, clusters)), dma((clusters,)), dma((clusters,)), dma((bands,)), dma((bands,)),
+            dma((2,)), dma((2, clusters)), dma((clusters,)), dma((clusters,)), dma((bands,)), dma((bands,)),
         ],
         compiler_params=pltpu.CompilerParams(collective_id=0, has_side_effects=True),
         name="detect",
-    )(disturbance_variance, propagation_gains, observed_samples, retained_branches)
+    )(disturbance_variance.T, propagation_gains, observed_samples, retained_branches)
 
 
 def solution(mesh):

time: 24.4 us -> 20.6 us (0.84)
  Pallas kernels: 21.3 us -> 18.8 us
  local copies, waits for them, and re-layouts: 2.9 us -> 1.57 us
    pallas_call x1, Pallas kernels: 21.3 us -> 18.8 us  [local(): pl.pallas_call(functools.partial(kernel, dims), out_shape=jax.ShapeDtypeS...]
    unnamed x2 -> x1, local copies, waits for them, and re-layouts: 2.9 us -> 1.57 us
where the time goes in v2:
time: 20.6 us; the launch traced here: 20.4 us
  Pallas kernels  18.8 us (91%)
  local copies, waits for them, and re-layouts  1.57 us (8%)
    pallas_call x1, Pallas kernels, local(): pl.pallas_call(functools.partial(kernel, dims), out_shape=jax.ShapeDtypeS...  18.8 us
    unnamed x1, local copies, waits for them, and re-layouts  1.57 us

profile of v2, /device:TPU:0, one launch (start us, length us, event | category | flops | bytes accessed | tf_op | source)
XLA Modules:
  0.0 20.4 jit_solution(10498011971807719796)
XLA Ops:
  0.0 18.8 %detect.1 = f32[4,2,4,1024]{3,2,1,0:T(4,128)} custom-call(f32[2,4]{1,0:T(2,128)} %bitcast.1, bf16[1,16,64,1024]{3,2,1,0:T(8,128)(2,1)} %gains_ref.1, bf16[1,16,32,1024]{3,2,1,0:T(8,128)(2,1)} %samples_ref.1, s32[4,2,4,1024]{3,2,1,0:T(4,128)} %branches_any.1), custom_call_target="tpu_custom_call" | custom-call | tf_op jit(solution)/shard_map/detect/pallas_call | solution.py:250
  18.9 1.6 %copy.6 = f32[4,2,4,1024]{3,2,1,0:T(4,128)} copy(f32[4,2,4,1024]{3,2,1,0:T(4,128)} %detect.1) | data formatting | bytes 262144
